TPU v7x, 32 devices: a whole 2x2x4 slice. The times are simulated.
32 devices in a mesh: dp: 2 (over x), fsdp: 4 (over z), sp: 4 (over y, core).
Axes of the slice: x: 2, y: 2, z: 4, core: 2. Of those that a mesh axis runs over, the one named last changes fastest.
Arguments:
- x_in: bfloat16 [96, 256, 2560], P(('dp', 'fsdp'), 'sp'), parts along dimension 0
- norm_attn: bfloat16 [2560], P('fsdp')
- w_query: bfloat16 [2560, 2560], P('fsdp')
- w_key: bfloat16 [2560, 2560], P('fsdp')
- w_value: bfloat16 [2560, 2560], P('fsdp')
- w_out: bfloat16 [2560, 2560], P('fsdp')
- norm_mlp: bfloat16 [2560], P('fsdp')
- w_gate: bfloat16 [2560, 6912], P('fsdp')
- w_up: bfloat16 [2560, 6912], P('fsdp')
- w_down: bfloat16 [6912, 2560], P('fsdp')
Outputs:
- output: bfloat16 [96, 256, 2560], P(('dp', 'fsdp'), 'sp'), parts along dimension 0
There are 2 independent parts. A program takes and returns all parts, laid end to end along the dimension named above; an argument that names none is the same for every part.
All inputs are finite; a program needn't handle non-finite values.
Results may differ from a plain program's by a relative error of at most 0.0114395.
Values are sent between devices in bfloat16 or wider.
A program may use at most 1 GiB of HBM per device.

v0:
```python
import math
import functools
import jax
import jax.numpy as jnp
from jax import lax
from jax.sharding import PartitionSpec as P

HEAD_DIM = 128
NORM_EPS = 1e-5
ROPE_THETA = 5e7
MASK_VALUE = -1e30


def rms_norm(hidden, gain):
    hid_f32 = hidden.astype(jnp.float32)
    inv_rms = lax.rsqrt(jnp.mean(hid_f32 * hid_f32, axis=-1, keepdims=True) + NORM_EPS)
    return (hid_f32 * inv_rms * gain.astype(jnp.float32)).astype(jnp.bfloat16)


def apply_rope(proj, angles):
    half_dim = proj.shape[-1] // 2
    lower_half = proj[..., :half_dim]
    upper_half = proj[..., half_dim:]
    cos_tab = jnp.cos(angles)[..., None, :]
    sin_tab = jnp.sin(angles)[..., None, :]
    return jnp.concatenate([lower_half * cos_tab - upper_half * sin_tab, upper_half * cos_tab + lower_half * sin_tab], axis=-1)


def rope_angles(token_pos):
    inv_freq = jnp.exp(jnp.arange(HEAD_DIM // 2, dtype=jnp.float32) * (-2.0 * math.log(ROPE_THETA) / HEAD_DIM))
    return token_pos.astype(jnp.float32)[:, None] * inv_freq[None, :]


def gather_weight(weight_shard):
    return lax.all_gather(weight_shard, 'fsdp', axis=0, tiled=True)


def local_layer(x_loc, norm_attn, w_query, w_key, w_value, w_out, norm_mlp, w_gate, w_up, w_down, num_shards):
    num_rows, shard_len, model_dim = x_loc.shape
    head_shape = (num_rows, shard_len, model_dim // HEAD_DIM, HEAD_DIM)
    pos_loc = jnp.arange(shard_len, dtype=jnp.int32) * num_shards + lax.axis_index('sp')
    seq_idx = jnp.arange(num_shards * shard_len, dtype=jnp.int32)
    pos_all = (seq_idx % shard_len) * num_shards + seq_idx // shard_len
    angles = rope_angles(pos_loc)
    normed = rms_norm(x_loc, gather_weight(norm_attn))
    query_rot = apply_rope(jnp.dot(normed, gather_weight(w_query), preferred_element_type=jnp.float32).reshape(head_shape), angles).astype(jnp.bfloat16)
    key_rot = apply_rope(jnp.dot(normed, gather_weight(w_key), preferred_element_type=jnp.float32).reshape(head_shape), angles).astype(jnp.bfloat16)
    value_loc = jnp.dot(normed, gather_weight(w_value), preferred_element_type=jnp.float32).astype(jnp.bfloat16).reshape(head_shape)
    key_all = lax.all_gather(key_rot, 'sp', axis=1, tiled=True)
    value_all = lax.all_gather(value_loc, 'sp', axis=1, tiled=True)
    scores = jnp.einsum('bqhd,bkhd->bhqk', query_rot, key_all, preferred_element_type=jnp.float32) * HEAD_DIM ** -0.5
    allowed = pos_all[None, None, None, :] <= pos_loc[None, None, :, None]
    attn_prob = jax.nn.softmax(jnp.where(allowed, scores, MASK_VALUE), axis=-1).astype(jnp.bfloat16)
    attn_mix = jnp.einsum('bhqk,bkhd->bqhd', attn_prob, value_all, preferred_element_type=jnp.float32).astype(jnp.bfloat16).reshape(num_rows, shard_len, model_dim)
    resid = (x_loc.astype(jnp.float32) + jnp.dot(attn_mix, gather_weight(w_out), preferred_element_type=jnp.float32)).astype(jnp.bfloat16)
    normed_mlp = rms_norm(resid, gather_weight(norm_mlp))
    gate_act = jax.nn.silu(jnp.dot(normed_mlp, gather_weight(w_gate), preferred_element_type=jnp.float32))
    up_proj = jnp.dot(normed_mlp, gather_weight(w_up), preferred_element_type=jnp.float32)
    hidden_mlp = (gate_act * up_proj).astype(jnp.bfloat16)
    return (resid.astype(jnp.float32) + jnp.dot(hidden_mlp, gather_weight(w_down), preferred_element_type=jnp.float32)).astype(jnp.bfloat16)


def solution(mesh):
    row_spec = P(('dp', 'fsdp'), 'sp', None)
    weight_spec = P('fsdp', None)
    gain_spec = P('fsdp')
    in_specs = (row_spec, gain_spec, weight_spec, weight_spec, weight_spec, weight_spec, gain_spec, weight_spec, weight_spec, weight_spec)
    layer_fn = functools.partial(local_layer, num_shards=mesh.shape['sp'])
    return jax.shard_map(layer_fn, mesh=mesh, in_specs=in_specs, out_specs=row_spec, check_vma=False)
```

profile of v0, /device:TPU:0, one launch (start us, length us, event | category | flops | bytes accessed | tf_op | source)
XLA Modules:
  0.0 2949.3 jit_solution(14721656314706254423)
XLA Ops:
  6.5 0.0 all-gather.16.cloned.1.call-start
  6.5 0.7 all-gather.16.cloned.1.call-update
  7.3 0.0 all-gather.18.cloned.1.call-start
  7.3 0.7 all-gather.18.cloned.1.call-update
  8.0 0.0 all-gather.12.cloned.1.call-start
  8.1 0.7 all-gather.12.cloned.1.call-update
  8.7 0.0 all-gather.20.cloned.1.call-start
  8.8 14.8 all-gather
  23.7 3.0 fusion.21
  26.6 0.2 multiply_cosine_fusion
  26.8 212.1 %all-gather.16.cloned.1.call-done = bf16[2560,2560]{1,0:T(8,128)(2,1)} async-done(((bf16[640,2560]{1,0:T(8,128)(2,1)}), bf16[2560,2560]{1,0:T(8,128)(2,1)}) %all-gather.16.cloned.1.call-update) | async-done | bytes 13107216 | tf_op jit(solution)/shard_map/all_gather | solution.py:35
  239.0 16.5 fusion.15
  255.5 9.1 reshape.156
  264.7 201.4 %all-gather.18.cloned.1.call-done = bf16[2560,2560]{1,0:T(8,128)(2,1)} async-done(((bf16[640,2560]{1,0:T(8,128)(2,1)}), bf16[2560,2560]{1,0:T(8,128)(2,1)}) %all-gather.18.cloned.1.call-update) | async-done | bytes 13107216 | tf_op jit(solution)/shard_map/all_gather | solution.py:35
  466.1 16.5 fusion.13
  482.6 9.2 reshape.157
  491.8 29.4 fusion.71
  521.1 20.9 subtract_convert_fusion.1
  542.0 4.1 pad_maximum_fusion.1
  546.1 0.0 all-gather.20.cloned.1.call-update
  546.1 0.0 all-gather.14.cloned.1.call-start
  546.2 146.9 %all-gather.12.cloned.1.call-done = bf16[2560,2560]{1,0:T(8,128)(2,1)} async-done(((bf16[640,2560]{1,0:T(8,128)(2,1)}), bf16[2560,2560]{1,0:T(8,128)(2,1)}) %all-gather.12.cloned.1.call-update) | async-done | bytes 13107216 | tf_op jit(solution)/shard_map/all_gather | solution.py:35
  693.1 14.6 fusion.52
  707.8 3.0 copy.49
  710.8 0.0 all-gather.14.cloned.1.call-update
  710.8 0.0 all-gather.22.cloned.1.call-start
  710.9 0.5 all-gather.22.cloned.1.call-update
  711.4 0.0 all-gather.24.cloned.1.call-start
  711.5 0.7 all-gather.24.cloned.1.call-update
  712.2 0.0 copy-start.1
  712.2 0.0 all-gather.26.cloned.1.call-start
  712.2 0.7 all-gather.26.cloned.1.call-update
  712.9 0.0 all-gather.28.cloned.1.call-start
  713.0 0.7 all-gather.28.cloned.1.call-update
  713.7 13.0 all-gather.1
  726.8 0.1 broadcast_compare_fusion
  726.9 66.8 %all-gather.20.cloned.1.call-done = bf16[12,256,20,128]{3,1,2,0:T(8,128)(2,1)} async-done(((bf16[12,64,20,128]{3,1,2,0:T(8,128)(2,1)}), bf16[12,256,20,128]{3,1,2,0:T(8,128)(2,1)}) %all-gather.20.cloned.1.call-update) | async-done | bytes 15728656 | tf_op jit(solution)/shard_map/all_gather | solution.py:49
  793.6 18.0 fusion.73
  811.7 84.3 %all-gather.14.cloned.1.call-done = bf16[12,256,20,128]{3,1,2,0:T(8,128)(2,1)} async-done(((bf16[12,64,20,128]{3,1,2,0:T(8,128)(2,1)}), bf16[12,256,20,128]{3,1,2,0:T(8,128)(2,1)}) %all-gather.14.cloned.1.call-update) | async-done | bytes 15728656 | tf_op jit(solution)/shard_map/all_gather | solution.py:50
  896.0 14.2 convert_bitcast_fusion
  910.2 214.6 %all-gather.22.cloned.1.call-done = bf16[2560,2560]{1,0:T(8,128)(2,1)} async-done(((bf16[640,2560]{1,0:T(8,128)(2,1)}), bf16[2560,2560]{1,0:T(8,128)(2,1)}) %all-gather.22.cloned.1.call-update) | async-done | bytes 13107216 | tf_op jit(solution)/shard_map/all_gather | solution.py:35
  1124.8 16.6 fusion.25
  1141.3 576.9 %all-gather.24.cloned.1.call-done = bf16[2560,6912]{1,0:T(8,128)(2,1)} async-done(((bf16[640,6912]{1,0:T(8,128)(2,1)}), bf16[2560,6912]{1,0:T(8,128)(2,1)}) %all-gather.24.cloned.1.call-update) | async-done | bytes 35389456 | tf_op jit(solution)/shard_map/all_gather | solution.py:35
  1718.2 36.8 %fusion.5 = f32[12,64,6912]{2,1,0:T(8,128)} fusion(bf16[2560,6912]{1,0:T(8,128)(2,1)} %all-gather.24.cloned.1.call-done, bf16[12,64,2560]{2,1,0:T(8,128)(2,1)} %get-tuple-element.20, f32[2560]{0:T(1024)S(1)} %reshape.164, f32[12,64]{1,0:T(8,128)S(1)} %add_rsqrt_fusion), kind=kOutput, calls=%fused_computation.5 | convolution fusion | flops 27186954240 | bytes 60568576 | tf_op jit(solution)/shard_map/dot_general | solution.py:57
  1755.0 557.5 %all-gather.26.cloned.1.call-done = bf16[2560,6912]{1,0:T(8,128)(2,1)} async-done(((bf16[640,6912]{1,0:T(8,128)(2,1)}), bf16[2560,6912]{1,0:T(8,128)(2,1)}) %all-gather.26.cloned.1.call-update) | async-done | bytes 35389456 | tf_op jit(solution)/shard_map/all_gather | solution.py:35
  2312.5 38.1 %multiply_convert_fusion.clone.6 = bf16[12,64,6912]{2,1,0:T(8,128)(2,1)} fusion(f32[12,64,6912]{2,1,0:T(8,128)} %fusion.5, bf16[2560,6912]{1,0:T(8,128)(2,1)} %all-gather.26.cloned.1.call-done, bf16[12,64,2560]{2,1,0:T(8,128)(2,1)} %get-tuple-element.20, f32[2560]{0:T(1024)S(1)} %reshape.164, f32[12,64]{1,0:T(8,128)S(1)} %add_rsqrt_fusion), kind=kOutput, calls=%fused_computation.7.clone.clone.clone.clone.clone.1 | convolution fusion | flops 27218804736 | bytes 71185408 | tf_op jit(solution)/shard_map/dot_general | solution.py:58
  2350.6 556.3 %all-gather.28.cloned.1.call-done = bf16[6912,2560]{1,0:T(8,128)(2,1)} async-done(((bf16[1728,2560]{1,0:T(8,128)(2,1)}), bf16[6912,2560]{1,0:T(8,128)(2,1)}) %all-gather.28.cloned.1.call-update) | async-done | bytes 35389456 | tf_op jit(solution)/shard_map/all_gather | solution.py:35
  2906.9 35.4 %fusion.28 = bf16[12,64,2560]{2,1,0:T(8,128)(2,1)} fusion(bf16[12,64,2560]{2,1,0:T(8,128)(2,1)} %get-tuple-element.20, bf16[6912,2560]{1,0:T(8,128)(2,1)} %all-gather.28.cloned.1.call-done, bf16[12,64,6912]{2,1,0:T(8,128)(2,1)} %multiply_convert_fusion.clone.6), kind=kOutput, calls=%fused_computation.34 | convolution fusion | flops 27184988160 | bytes 53870592 | tf_op jit(solution)/shard_map/dot_general | solution.py:60
  (15 shorter events, 0.2 us)
Async XLA Ops:
  6.5 2.3 copy-start
  6.5 232.5 %all-gather.16.cloned.1.call-start = ((), (), s32[]{:S(2)}) async-start(), calls=%async_computation.2 | async-start | bytes 16384000 | tf_op jit(solution)/shard_map/all_gather | solution.py:35
  7.3 458.8 %all-gather.18.cloned.1.call-start = ((), (), s32[]{:S(2)}) async-start(), calls=%async_computation.3 | async-start | bytes 16384000 | tf_op jit(solution)/shard_map/all_gather | solution.py:35
  8.0 685.1 %all-gather.12.cloned.1.call-start = ((), (), s32[]{:S(2)}) async-start(), calls=%async_computation | async-start | bytes 16384000 | tf_op jit(solution)/shard_map/all_gather | solution.py:35
  8.7 784.9 %all-gather.20.cloned.1.call-start = ((), (), s32[]{:S(2)}) async-start(), calls=%async_computation.4 | async-start | bytes 19660800 | tf_op jit(solution)/shard_map/all_gather | solution.py:49
  546.1 349.9 %all-gather.14.cloned.1.call-start = ((), (), s32[]{:S(2)}) async-start(), calls=%async_computation.1 | async-start | bytes 19660800 | tf_op jit(solution)/shard_map/all_gather | solution.py:50
  710.8 413.9 %all-gather.22.cloned.1.call-start = ((), (), s32[]{:S(2)}) async-start(), calls=%async_computation.5 | async-start | bytes 16384000 | tf_op jit(solution)/shard_map/all_gather | solution.py:35
  711.4 1006.8 %all-gather.24.cloned.1.call-start = ((), (), s32[]{:S(2)}) async-start(), calls=%async_computation.6 | async-start | bytes 44236800 | tf_op jit(solution)/shard_map/all_gather | solution.py:35
  712.2 1.5 copy-start.1
  712.2 1600.4 %all-gather.26.cloned.1.call-start = ((), (), s32[]{:S(2)}) async-start(), calls=%async_computation.7 | async-start | bytes 44236800 | tf_op jit(solution)/shard_map/all_gather | solution.py:35
  712.9 2194.0 %all-gather.28.cloned.1.call-start = ((), (), s32[]{:S(2)}) async-start(), calls=%async_computation.8 | async-start | bytes 44236800 | tf_op jit(solution)/shard_map/all_gather | solution.py:35
Sparse Core Ops, SparseCore 0:
  8.9 230.0 all-gather.15
  240.6 225.4 all-gather.17
  467.6 225.4 all-gather.11
  694.5 99.0 all-gather.19
  795.1 100.8 all-gather.13
  897.4 227.2 all-gather.21
  1126.3 591.8 all-gather.23
  1719.8 592.6 all-gather.25
  2314.1 592.6 all-gather.27
where the time goes:
time: 2960 us; the launch traced here: 2950 us
  waiting for transfers between devices  2620 us (89%)
  matrix products  207 us (7%)
  local copies, waits for them, and re-layouts  50.8 us (2%)
    all_gather x7, waiting for transfers between devices, gather_weight(): return lax.all_gather(weight_shard, 'fsdp', axis=0, tiled=True)  2470 us
    all_gather x1, waiting for transfers between devices, local_layer(): value_all = lax.all_gather(value_loc, 'sp', axis=1, tiled=True)  84.3 us
    all_gather x1, waiting for transfers between devices, local_layer(): key_all = lax.all_gather(key_rot, 'sp', axis=1, tiled=True)  66.8 us
  transfers between devices with their start and end apart: 9, of which 9 were waited for; matrix products, arithmetic and copies ran while one was open for 8% of the time, Pallas kernels for 0%

commit v1 on v0

v1 whole, which is shorter than its diff:
```python
import math
import functools
import jax
import jax.numpy as jnp
from jax import lax
from jax.experimental import pallas as pl
from jax.experimental.pallas import tpu as pltpu
from jax.sharding import PartitionSpec as P

HEAD_DIM = 128
NORM_EPS = 1e-5
ROPE_THETA = 5e7
MASK_VALUE = -1e30
MESH = pl.DeviceIdType.MESH
NZ = 4
SP = 4
PER = 3
BLK = 64
SEQ = SP * BLK
TOK = PER * SEQ
DIM = 2560
FFN = 6912
HALF = DIM // 2
TILE = 256
N_KINDS = 14
SLOTS = 8
AHEAD = 2
LAG = 3
W_Q, W_K, W_V, W_O, W_G, W_U, W_D = range(7)


def split_rows(block):
    over_z = block // 10 // 8 * 8
    over_x = (block - over_z) * 11 // 20 // 8 * 8
    return over_z, over_x


def remote(src, dst, send_sem, recv_sem, dev):
    return pltpu.make_async_remote_copy(
        src_ref=src, dst_ref=dst, send_sem=send_sem, recv_sem=recv_sem, device_id=dev, device_id_type=MESH)


class Mover:
    def __init__(self, shards, gathered, rounds, send_sem, recv_sem):
        self.shards, self.gathered, self.rounds = shards, gathered, rounds
        self.send_sem, self.recv_sem = send_sem, recv_sem
        dx, fz, s = lax.axis_index('dp'), lax.axis_index('fsdp'), lax.axis_index('sp')
        self.dx, self.fz, self.s = dx, fz, s
        self.y, self.c = lax.div(s, 2), lax.rem(s, 2)
        self.core_dev = (dx, fz, self.y * 2 + (1 - self.c))
        self.x_dev = (1 - dx, fz, s)
        self.y_dev = (dx, fz, (1 - self.y) * 2 + self.c)

    def block(self, dx, y, c):
        return (dx * 2 + y) * 2 + c

    def copies(self, r, stage):
        w, lo, width = self.rounds[r]
        sh, g = self.shards[w], self.gathered[w]
        rb = sh.shape[0] // 8
        cols = pl.ds(lo, width)
        az, ax = split_rows(rb)
        dx, y, c = self.dx, self.y, self.c
        mine = self.block(dx, y, c)
        diag = self.block(1 - dx, 1 - y, c)
        xblk, yblk = self.block(1 - dx, y, c), self.block(dx, 1 - y, c)
        slot = r % SLOTS
        out = []

        def rows(blk, a, b):
            return pl.ds(pl.multiple_of(blk * rb + a, 8), b - a)

        def add(kind, src, dst, dev):
            out.append(remote(src, dst, self.send_sem.at[slot, kind], self.recv_sem.at[slot, kind], dev))

        def same(kind, blk, a, b, dev):
            ref = g.at[1:NZ, rows(blk, a, b), cols]
            add(kind, ref, ref, dev)

        if stage == 'z':
            for k in range(1, NZ):
                dev = (dx, lax.rem(self.fz + k, NZ), self.s)
                add(k - 1, sh.at[rows(mine, 0, rb), cols], g.at[NZ - k, rows(mine, 0, rb), cols], dev)
                add(k + 2, sh.at[rows(diag, 0, az), cols], g.at[NZ - k, rows(diag, 0, az), cols], dev)
        if stage == 'p1':
            same(6, mine, 0, rb, self.x_dev)
            same(7, mine, 0, rb, self.y_dev)
        if stage == 'p1c':
            same(8, mine, 0, rb, self.core_dev)
        if stage == 'p2':
            same(9, yblk, az, az + ax, self.x_dev)
            same(10, xblk, az + ax, rb, self.y_dev)
        if stage == 'p2c':
            same(11, xblk, 0, rb, self.core_dev)
            same(12, yblk, 0, rb, self.core_dev)
        if stage == 'p3':
            same(13, diag, 0, rb, self.core_dev)
        return out

    def start(self, r, *stages):
        if 0 <= r < len(self.rounds):
            for stage in stages:
                for cp in self.copies(r, stage):
                    cp.start()

    def wait_recv(self, r, *stages):
        if 0 <= r < len(self.rounds):
            for stage in stages:
                for cp in self.copies(r, stage):
                    cp.wait_recv()

    def wait_send(self, r):
        if 0 <= r < len(self.rounds):
            for stage in ('z', 'p1', 'p1c', 'p2', 'p2c', 'p3'):
                for cp in self.copies(r, stage):
                    cp.wait_send()

    def step(self, i):
        if i == 0:
            for r in range(AHEAD):
                self.start(r, 'z')
        self.wait_send(i + AHEAD - SLOTS)
        self.start(i + AHEAD, 'z')
        self.wait_recv(i, 'z')
        self.start(i, 'p1', 'p1c')
        self.wait_recv(i - 1, 'p1')
        self.start(i - 1, 'p2', 'p2c')
        self.wait_recv(i - 2, 'p2')
        self.start(i - 2, 'p3')
        self.wait_recv(i - 3, 'p1c', 'p2c', 'p3')

    def ticks(self):
        return len(self.rounds) + LAG

    def finish(self):
        n = len(self.rounds)
        done = n + LAG + AHEAD - SLOTS
        for r in range(max(done, 0), n):
            self.wait_send(r)


def plan():
    rounds = []
    for half in range(2):
        rounds += [(w, half * HALF, HALF) for w in (W_Q, W_K, W_V)]
    rounds += [(W_O, 0, HALF), (W_O, HALF, HALF)]
    for c in range(9):
        rounds += [(W_G, c * 768, 768), (W_U, c * 768, 768)]
    lo = 0
    for width in (512, 512, 512, 512, 256, 256):
        rounds.append((W_D, lo, width))
        lo += width
    return rounds


def layer_kernel(rounds, x_loc, gain, cos_tab, sin_tab, keep, *refs):
    shards, refs = refs[:7], refs[7:]
    y_out, gathered, refs = refs[0], refs[1:8], refs[8:]
    (xg, act, big, mix, res, gbuf, wbuf, send_sem, recv_sem, x_send, x_recv, o_send, o_recv,
     g_send, g_recv, lsem, wsem, ysem) = refs
    mv = Mover(shards, gathered, rounds, send_sem, recv_sem)
    dx, fz, s = mv.dx, mv.fz, mv.s

    def at_rows(start, n):
        return pl.ds(pl.multiple_of(start, BLK), n)

    def x_copies():
        out = []
        for k in range(1, SP):
            t = lax.rem(s + k, SP)
            for b in range(PER):
                out.append(remote(x_loc.at[at_rows((PER * t + b) * BLK, BLK)], xg.at[at_rows(b * SEQ + s * BLK, BLK)],
                                  x_send.at[k - 1, b], x_recv.at[k - 1, b], (dx, fz, t)))
        return out

    def x_own():
        return [pltpu.make_async_copy(x_loc.at[at_rows((PER * s + b) * BLK, BLK)],
                                      xg.at[at_rows(b * SEQ + s * BLK, BLK)], lsem.at[b]) for b in range(PER)]

    def g_copies():
        return [remote(gain, gbuf.at[fz], g_send.at[k - 1], g_recv.at[k - 1], (dx, lax.rem(fz + k, NZ), s))
                for k in range(1, NZ)]

    def g_own():
        return pltpu.make_async_copy(gain, gbuf.at[fz], lsem.at[PER])

    def res_load():
        return pltpu.make_async_copy(x_loc, res, lsem.at[PER + 1])

    def o_copies(half):
        out = []
        cols = pl.ds(half * HALF, HALF)
        for k in range(1, SP):
            t = lax.rem(s + k, SP)
            for b in range(PER):
                out.append(remote(big.at[at_rows(b * SEQ + t * BLK, BLK), cols],
                                  mix.at[at_rows((PER * s + b) * BLK, BLK), cols],
                                  o_send.at[half, k - 1, b], o_recv.at[half, k - 1, b], (dx, fz, t)))
        return out

    def norm(src, row):
        gains = jnp.concatenate([gbuf[j, row:row + 1, :] for j in range(NZ)], axis=-1).astype(jnp.float32)

        def body(i, _):
            at = at_rows(i * BLK, BLK)
            h = src[at, :].astype(jnp.float32)
            inv = lax.rsqrt(jnp.mean(h * h, axis=-1, keepdims=True) + NORM_EPS)
            act[at, :] = (h * inv * gains).astype(jnp.bfloat16)
            return 0

        lax.fori_loop(0, TOK // BLK, body, 0)

    def loads(w, base, lo, slot, first):
        sh, g = shards[w], gathered[w]
        ks = sh.shape[0]
        cols = pl.ds(pl.multiple_of(lo, 128), TILE)
        out = []
        for j in range(NZ):
            src = sh.at[:, cols] if j == 0 else g.at[j, :, cols]
            at = pl.ds(pl.multiple_of(base + lax.rem(fz + j, NZ) * ks, 32), ks)
            out.append(pltpu.make_async_copy(src, wbuf.at[slot, at, :], wsem.at[slot, first + j]))
        return out

    def tiles(n, start, wait, compute):
        start(0, 0)

        def body(t, _):
            slot = lax.rem(t, 2)

            @pl.when(t + 1 < n)
            def _():
                start(t + 1, 1 - slot)

            wait(t, slot)
            compute(t, slot)
            return 0

        lax.fori_loop(0, n, body, 0)

    def simple(n, load, compute):
        def start(t, slot):
            for cp in load(t, slot):
                cp.start()

        def wait(t, slot):
            for cp in load(t, slot):
                cp.wait()

        tiles(n, start, wait, compute)

    m_rows = TOK // 2

    def by_rows(body):
        def go(m, _):
            body(pl.ds(pl.multiple_of(m * m_rows, m_rows), m_rows))
            return 0
        lax.fori_loop(0, TOK // m_rows, go, 0)

    def qkv(half):
        per = HALF // TILE

        def start(t, slot):
            for j, w in enumerate((W_Q, W_K, W_V)):
                @pl.when(lax.div(t, per) == j)
                def _():
                    for cp in loads(w, 0, half * HALF + lax.rem(t, per) * TILE, slot, 0):
                        cp.start()

        def wait(t, slot):
            for cp in loads(W_Q, 0, half * HALF + lax.rem(t, per) * TILE, slot, 0):
                cp.wait()

        def compute(t, slot):
            off = lax.div(t, per) * DIM + half * HALF + lax.rem(t, per) * TILE

            def body(at):
                acc = jnp.dot(act[at, :], wbuf[slot, 0:DIM, :], preferred_element_type=jnp.float32)

                @pl.when(t < 2 * per)
                def _():
                    cos, sin = cos_tab[at, :], sin_tab[at, :]
                    for h in range(TILE // HEAD_DIM):
                        p = acc[:, h * HEAD_DIM:(h + 1) * HEAD_DIM]
                        swapped = jnp.concatenate([p[:, HEAD_DIM // 2:], p[:, :HEAD_DIM // 2]], axis=-1)
                        rot = p * cos + swapped * sin
                        big[at, pl.ds(pl.multiple_of(off + h * HEAD_DIM, 128), HEAD_DIM)] = rot.astype(jnp.bfloat16)

                @pl.when(t >= 2 * per)
                def _():
                    big[at, pl.ds(pl.multiple_of(off, 128), TILE)] = acc.astype(jnp.bfloat16)

            by_rows(body)

        tiles(3 * per, start, wait, compute)

    def attention(half):
        n = HALF // HEAD_DIM

        def body(h, _):
            col = half * HALF + h * HEAD_DIM
            for b in range(PER):
                at = pl.ds(b * SEQ, SEQ)
                q, k, v = (big[at, pl.ds(pl.multiple_of(col + j * DIM, 128), HEAD_DIM)] for j in range(3))
                sc = lax.dot_general(q, k, (((1,), (1,)), ((), ())), preferred_element_type=jnp.float32)
                sc = jnp.where(keep[...] > 0, sc * HEAD_DIM ** -0.5, MASK_VALUE)
                e = jnp.exp(sc - jnp.max(sc, axis=-1, keepdims=True))
                tot = jnp.sum(e, axis=-1, keepdims=True)
                o = jnp.dot(e.astype(jnp.bfloat16), v, preferred_element_type=jnp.float32) / tot
                big[at, pl.ds(pl.multiple_of(col, 128), HEAD_DIM)] = o.astype(jnp.bfloat16)
            return 0

        lax.fori_loop(0, n, body, 0)

    def send_mix(half):
        for cp in o_copies(half):
            cp.start()
        cols = pl.ds(half * HALF, HALF)
        for b in range(PER):
            mix[at_rows((PER * s + b) * BLK, BLK), cols] = big[at_rows(b * SEQ + s * BLK, BLK), cols]

    def out_proj():
        for half in range(2):
            for cp in o_copies(half):
                cp.wait_recv()

        def load(t, slot):
            return loads(W_O, 0, t * TILE, slot, 0)

        def compute(t, slot):
            cols = pl.ds(pl.multiple_of(t * TILE, 128), TILE)

            def body(at):
                acc = jnp.dot(mix[at, :], wbuf[slot, 0:DIM, :], preferred_element_type=jnp.float32)
                res[at, cols] = (res[at, cols].astype(jnp.float32) + acc).astype(jnp.bfloat16)

            by_rows(body)

        simple(DIM // TILE, load, compute)
        norm(res, 1)
        for half in range(2):
            for cp in o_copies(half):
                cp.wait_send()

    def gate_up(lo, width):
        def load(t, slot):
            return loads(W_G, 0, lo + t * TILE, slot, 0) + loads(W_U, DIM, lo + t * TILE, slot, NZ)

        def compute(t, slot):
            def body(at):
                a = act[at, :]
                g = jnp.dot(a, wbuf[slot, 0:DIM, :], preferred_element_type=jnp.float32)
                u = jnp.dot(a, wbuf[slot, DIM:2 * DIM, :], preferred_element_type=jnp.float32)
                big[at, pl.ds(pl.multiple_of(lo + t * TILE, 128), TILE)] = (g / (1.0 + jnp.exp(-g)) * u).astype(jnp.bfloat16)

            by_rows(body)

        simple(width // TILE, load, compute)

    def y_copy(t):
        cols = pl.ds(pl.multiple_of(t * TILE, 128), TILE)
        return pltpu.make_async_copy(xg.at[:, cols], y_out.at[:, cols], ysem.at[t])

    def down(lo, width):
        def load(t, slot):
            return loads(W_D, 0, lo + t * TILE, slot, 0)

        def compute(t, slot):
            cols = pl.ds(pl.multiple_of(lo + t * TILE, 128), TILE)

            def body(at):
                acc = jnp.dot(big[at, 0:FFN], wbuf[slot, 0:FFN, :], preferred_element_type=jnp.float32)
                xg[at, cols] = (res[at, cols].astype(jnp.float32) + acc).astype(jnp.bfloat16)

            by_rows(body)
            y_copy(lo // TILE + t).start()

        simple(width // TILE, load, compute)

    def first_norm():
        for cp in x_copies() + g_copies():
            cp.wait_recv()
        for cp in x_own():
            cp.wait()
        g_own().wait()
        norm(xg, 0)

    def late_sends():
        for cp in x_copies() + g_copies():
            cp.wait_send()
        res_load().wait()

    for cp in x_copies() + g_copies() + x_own() + [g_own(), res_load()]:
        cp.start()
    hooks = {}

    def hook(tick, fn):
        hooks.setdefault(tick, []).append(fn)

    last = {}
    for r, (w, lo, width) in enumerate(rounds):
        last[(w, lo)] = r + LAG
    hook(3, first_norm)
    hook(4, late_sends)
    for half in range(2):
        tick = last[(W_V, half * HALF)]
        hook(tick, functools.partial(qkv, half))
        hook(tick + 1, functools.partial(attention, half))
        hook(tick + 1, functools.partial(send_mix, half))
    hook(max(last[(W_O, HALF)], last[(W_V, HALF)] + 2), out_proj)
    for w, lo, width in rounds:
        if w == W_U:
            hook(last[(w, lo)], functools.partial(gate_up, lo, width))
        if w == W_D:
            hook(last[(w, lo)], functools.partial(down, lo, width))
    for i in range(mv.ticks()):
        mv.step(i)
        for fn in hooks.get(i, ()):
            fn()
    for t in range(DIM // TILE):
        y_copy(t).wait()
    mv.finish()


def local_layer(x_loc, norm_attn, w_query, w_key, w_value, w_out, norm_mlp, w_gate, w_up, w_down):
    shards = (w_query, w_key, w_value, w_out, w_gate, w_up, w_down)
    gain = jnp.concatenate([norm_attn[None], norm_mlp[None], jnp.zeros((14, DIM // NZ), jnp.bfloat16)], axis=0)
    seq_idx = jnp.arange(SEQ, dtype=jnp.int32)
    pos = (seq_idx % BLK) * SP + seq_idx // BLK
    inv_freq = jnp.exp(jnp.arange(HEAD_DIM // 2, dtype=jnp.float32) * (-2.0 * math.log(ROPE_THETA) / HEAD_DIM))
    angles = pos.astype(jnp.float32)[:, None] * inv_freq[None, :]
    cos, sin = jnp.cos(angles), jnp.sin(angles)
    cos_tab = jnp.tile(jnp.concatenate([cos, cos], axis=-1), (PER, 1))
    sin_tab = jnp.tile(jnp.concatenate([-sin, sin], axis=-1), (PER, 1))
    keep = (pos[None, :] <= pos[:, None]).astype(jnp.float32)
    rounds = plan()
    any_spec = pl.BlockSpec(memory_space=pl.ANY)
    vmem_spec = pl.BlockSpec(memory_space=pltpu.VMEM)
    dma = pltpu.SemaphoreType.DMA
    bf16 = jnp.bfloat16
    outs = [jax.ShapeDtypeStruct((TOK, DIM), bf16)]
    outs += [jax.ShapeDtypeStruct((NZ,) + w.shape, bf16) for w in shards]
    res = pl.pallas_call(
        functools.partial(layer_kernel, rounds),
        out_shape=outs,
        in_specs=[any_spec, any_spec] + [vmem_spec] * 3 + [any_spec] * 7,
        out_specs=[any_spec] * 8,
        scratch_shapes=[
            pltpu.VMEM((TOK, DIM), bf16), pltpu.VMEM((TOK, DIM), bf16), pltpu.VMEM((TOK, 3 * DIM), bf16),
            pltpu.VMEM((TOK, DIM), bf16), pltpu.VMEM((TOK, DIM), bf16), pltpu.VMEM((NZ, 16, DIM // NZ), bf16),
            pltpu.VMEM((2, FFN, TILE), bf16),
            dma((SLOTS, N_KINDS)), dma((SLOTS, N_KINDS)), dma((SP - 1, PER)), dma((SP - 1, PER)),
            dma((2, SP - 1, PER)), dma((2, SP - 1, PER)), dma((NZ - 1,)), dma((NZ - 1,)),
            dma((PER + 2,)), dma((2, 2 * NZ)), dma((DIM // TILE,))],
        compiler_params=pltpu.CompilerParams(has_side_effects=True, vmem_limit_bytes=60 * 1024 * 1024),
    )(x_loc.reshape(TOK, DIM), gain, cos_tab, sin_tab, keep, *shards)
    return res[0].reshape(x_loc.shape)


def solution(mesh):
    row_spec = P(('dp', 'fsdp'), 'sp', None)
    weight_spec = P('fsdp', None)
    gain_spec = P('fsdp')
    in_specs = (row_spec, gain_spec, weight_spec, weight_spec, weight_spec, weight_spec, gain_spec, weight_spec, weight_spec, weight_spec)
    return jax.shard_map(local_layer, mesh=mesh, in_specs=in_specs, out_specs=row_spec, check_vma=False)
```

time: 2960 us -> 653 us (0.22)
  the two profiles are of different devices: /device:TPU:0 before, /device:TPU:29 now
where the time goes in v1:
time: 653 us
  Pallas kernels  643 us (98%)
  local copies, waits for them, and re-layouts  7.29 us (1%)
    pallas_call x1, Pallas kernels, local_layer(): pl.pallas_call(functools.partial(layer_kernel, rounds), out_shape=outs, i...  643 us

profile of v1, /device:TPU:29, one launch (start us, length us, event | category | flops | bytes accessed | tf_op | source)
XLA Modules:
  0.0 652.8 jit_solution(17314480755831062627)
XLA Ops:
  0.0 0.1 pad.6.clone
  0.1 0.7 broadcast_in_dim.6
  0.8 0.7 broadcast_in_dim.14
  1.5 0.7 maximum_maximum_fusion.gain
  2.2 0.8 compare_convert_fusion.keep
  3.0 0.5 fusion
  3.5 0.1 pad_maximum_fusion
  3.7 0.8 tile.8
  4.4 0.8 tile.20
  5.2 643.3 %shard_map.100 = (bf16[768,2560]{1,0:T(8,128)(2,1)}, bf16[4,640,2560]{2,1,0:T(8,128)(2,1)}, bf16[4,640,2560]{2,1,0:T(8,128)(2,1)}, bf16[4,640,2560]{2,1,0:T(8,12...) custom-call(bf16[768,2560]{1,0:T(8,128)(2,1)} %bitcast.5, ...), custom_call_target="tpu_custom_call" | custom-call | tf_op jit(solution)/shard_map/pallas_call | solution.py:442
  648.5 4.3 copy.12
  (4 shorter events, 0.0 us)

commit v2 on v1

v2 whole, which is shorter than its diff:
```python
import math
import functools
import jax
import jax.numpy as jnp
from jax import lax
from jax.experimental import pallas as pl
from jax.experimental.pallas import tpu as pltpu
from jax.sharding import PartitionSpec as P

HEAD_DIM = 128
NORM_EPS = 1e-5
ROPE_THETA = 5e7
MASK_VALUE = -1e30
MESH = pl.DeviceIdType.MESH
NZ = 4
SP = 4
ROWS = 12
BLK = 64
SEQ = SP * BLK
TOK = ROWS * BLK
ALL = ROWS * SEQ
DIM = 2560
FFN = 6912
HALF = DIM // 2
OWN = DIM // SP
HEADS = OWN // 128
PARTS = 3
OUT_WAIT = 1
EARLY = 13
FORWARD_TICKS = (2, 4, 6, 7)
GATE_WIDTHS = (1536, 1536, 1280, 1280, 768, 512)
DOWN_WIDTHS = (768, 768, 512, 256, 256)
TILE = 256
N_KINDS = 16
SLOTS = 12
AHEAD = 3
LAG = 5
Z_STAGES = ('z1', 'z2', 'z3')
W_Q, W_K, W_V, W_O, W_G, W_U, W_D = range(7)


def split_rows(block, early):
    if early:
        over_z = block // 16 * 8
        return over_z, block - over_z
    over_z = block // 24 * 8
    return over_z, (block - over_z) // 16 * 8 + (8 if block % 24 else 0)


def remote(src, dst, send_sem, recv_sem, dev):
    return pltpu.make_async_remote_copy(
        src_ref=src, dst_ref=dst, send_sem=send_sem, recv_sem=recv_sem, device_id=dev, device_id_type=MESH)


class Mover:
    def __init__(self, shards, gathered, rounds, early, send_sem, recv_sem):
        self.early = early
        self.shards, self.gathered, self.rounds = shards, gathered, rounds
        self.send_sem, self.recv_sem = send_sem, recv_sem
        dx, fz, s = lax.axis_index('dp'), lax.axis_index('fsdp'), lax.axis_index('sp')
        self.dx, self.fz, self.s = dx, fz, s
        self.y, self.c = lax.div(s, 2), lax.rem(s, 2)
        self.core_dev = (dx, fz, self.y * 2 + (1 - self.c))
        self.x_dev = (1 - dx, fz, s)
        self.y_dev = (dx, fz, (1 - self.y) * 2 + self.c)

    def block(self, dx, y, c):
        return (dx * 2 + y) * 2 + c

    def copies(self, r, stage):
        w, lo, width = self.rounds[r]
        sh, g = self.shards[w], self.gathered[w]
        rb = sh.shape[0] // 8
        cols = pl.ds(lo, width)
        az, ax = split_rows(rb, r < self.early)
        dx, y, c = self.dx, self.y, self.c
        mine = self.block(dx, y, c)
        diag = self.block(1 - dx, 1 - y, c)
        xblk, yblk = self.block(1 - dx, y, c), self.block(dx, 1 - y, c)
        slot = r % SLOTS
        out = []

        def rows(blk, a, b):
            return pl.ds(pl.multiple_of(blk * rb + a, 8), b - a)

        def add(kind, src, dst, dev):
            out.append(remote(src, dst, self.send_sem.at[slot, kind], self.recv_sem.at[slot, kind], dev))

        def same(kind, blk, a, b, dev):
            if a == b:
                return
            ref = g.at[1:NZ, rows(blk, a, b), cols]
            add(kind, ref, ref, dev)

        if w <= W_V:
            at = pl.ds(pl.multiple_of(dx * (DIM // 8), 8), DIM // 8)
            cols = pl.ds(pl.multiple_of(self.s * OWN + lo, 128), width)
            if stage in Z_STAGES:
                k = int(stage[1])
                add(k - 1, sh.at[at, cols], g.at[NZ - k, at, cols], (dx, lax.rem(self.fz + k, NZ), self.s))
            if stage == 'zf':
                low = self.fz < NZ // 2
                add(14, g.at[2, at, cols], g.at[jnp.where(low, NZ - 1, 1), at, cols],
                    (dx, jnp.where(low, 0, NZ - 1), self.s))
            if stage == 'p1':
                ref = g.at[1:NZ, at, cols]
                add(6, ref, ref, self.x_dev)
            return out
        if stage in Z_STAGES:
            k = int(stage[1])
            dev = (dx, lax.rem(self.fz + k, NZ), self.s)
            add(k - 1, sh.at[rows(mine, 0, rb), cols], g.at[NZ - k, rows(mine, 0, rb), cols], dev)
            add(k + 2, sh.at[rows(diag, 0, az), cols], g.at[NZ - k, rows(diag, 0, az), cols], dev)
        if stage == 'zf':
            low = self.fz < NZ // 2
            dev = (dx, jnp.where(low, 0, NZ - 1), self.s)
            there = jnp.where(low, NZ - 1, 1)
            for kind, blk, top in ((14, mine, rb), (15, diag, az)):
                add(kind, g.at[2, rows(blk, 0, top), cols], g.at[there, rows(blk, 0, top), cols], dev)
        if stage == 'p1':
            same(6, mine, 0, rb, self.x_dev)
            same(7, mine, 0, rb, self.y_dev)
        if stage == 'p1c':
            same(8, mine, 0, rb, self.core_dev)
        if stage == 'p2':
            same(9, yblk, az, az + ax, self.x_dev)
            same(10, xblk, az + ax, rb, self.y_dev)
        if stage == 'p2c':
            same(11, xblk, 0, rb, self.core_dev)
            same(12, yblk, 0, rb, self.core_dev)
        if stage == 'p3':
            same(13, diag, 0, rb, self.core_dev)
        return out

    def when_send(self, stage):
        if stage == 'z1':
            return self.fz != NZ - 1
        if stage == 'z3':
            return self.fz != 0
        if stage == 'zf':
            return jnp.logical_and(self.fz != 0, self.fz != NZ - 1)
        return None

    def when_recv(self, stage):
        if stage == 'z1':
            return self.fz != 0
        if stage == 'z3':
            return self.fz != NZ - 1
        if stage == 'zf':
            return jnp.logical_or(self.fz == 0, self.fz == NZ - 1)
        return None

    def each(self, r, stages, when, act):
        if 0 <= r < len(self.rounds):
            for stage in stages:
                cond = when(stage)

                def go():
                    for cp in self.copies(r, stage):
                        act(cp)

                if cond is None:
                    go()
                else:
                    pl.when(cond)(go)

    def start(self, r, *stages):
        self.each(r, stages, self.when_send, lambda cp: cp.start())

    def wait_recv(self, r, *stages):
        self.each(r, stages, self.when_recv, lambda cp: cp.wait_recv())

    def wait_send(self, r):
        self.each(r, Z_STAGES + ('zf', 'p1', 'p1c', 'p2', 'p2c', 'p3'), self.when_send, lambda cp: cp.wait_send())

    def step(self, i):
        if i == 0:
            for r in range(AHEAD):
                self.start(r, *Z_STAGES)
        self.wait_send(i + AHEAD - SLOTS)
        self.start(i + AHEAD, *Z_STAGES)
        self.wait_recv(i, *Z_STAGES)
        self.start(i, 'zf')
        self.wait_recv(i, 'zf')
        self.start(i, 'p1', 'p1c')
        self.wait_recv(i - 2, 'p1')
        self.start(i - 2, 'p2', 'p2c')
        self.wait_recv(i - 4, 'p2')
        self.start(i - 4, 'p3')
        self.wait_recv(i - 5, 'p1c', 'p2c', 'p3')

    def ticks(self):
        return len(self.rounds) + LAG

    def finish(self):
        n = len(self.rounds)
        done = n + LAG + AHEAD - SLOTS
        for r in range(max(done, 0), n):
            self.wait_send(r)


def plan():
    rounds = []

    def add(weights, widths):
        lo = 0
        for width in widths:
            rounds.extend((w, lo, width) for w in weights)
            lo += width

    add((W_Q,), (128, 256, 256))
    add((W_K,), (256, 384))
    add((W_V,), (256, 384))
    add((W_O,), (HALF, HALF))
    add((W_G, W_U), GATE_WIDTHS)
    add((W_D,), DOWN_WIDTHS)
    return rounds, EARLY


def layer_kernel(rounds, early, x_loc, gain, cos_tab, sin_tab, keep, *refs):
    shards, refs = refs[:7], refs[7:]
    y_out, gathered, refs = refs[0], refs[1:8], refs[8:]
    (xa, big, mix, res, gbuf, wbuf, send_sem, recv_sem, x_send, x_recv, o_send, o_recv,
     g_send, g_recv, lsem, wsem, ysem) = refs
    mv = Mover(shards, gathered, rounds, early, send_sem, recv_sem)
    dx, fz, s = mv.dx, mv.fz, mv.s
    s_y = (1 - mv.y) * 2 + mv.c
    per = ROWS // PARTS

    def at_rows(start, n):
        return pl.ds(pl.multiple_of(start, BLK), n)

    def for_each(lo, hi, body):
        def go(b, _):
            body(b)
            return 0
        lax.fori_loop(lo, hi, go, 0)

    def x_copy(k, b):
        mine, theirs = at_rows(b * SEQ + s * BLK, BLK), at_rows(b * SEQ + s_y * BLK, BLK)
        here = x_loc.at[at_rows(b * BLK, BLK)]
        src, dst, dev = ((here, xa.at[mine], mv.y_dev), (here, xa.at[mine], mv.core_dev),
                         (xa.at[theirs], xa.at[theirs], mv.core_dev))[k]
        return remote(src, dst, x_send.at[k, b], x_recv.at[k, b], dev)

    def x_own(b):
        return pltpu.make_async_copy(x_loc.at[at_rows(b * BLK, BLK)], xa.at[at_rows(b * SEQ + s * BLK, BLK)], lsem.at[b])

    def g_copies():
        return [remote(gain, gbuf.at[fz], g_send.at[k - 1], g_recv.at[k - 1], (dx, lax.rem(fz + k, NZ), s))
                for k in range(1, NZ)]

    def g_own():
        return pltpu.make_async_copy(gain, gbuf.at[fz], lsem.at[ROWS])

    def res_load():
        return pltpu.make_async_copy(x_loc, res, lsem.at[ROWS + 1])

    def o_copy(k, b):
        t = lax.rem(s + k, SP)
        return remote(big.at[at_rows(b * SEQ + t * BLK, BLK), 0:OWN],
                      mix.at[at_rows(b * BLK, BLK), pl.ds(pl.multiple_of(s * OWN, 128), OWN)],
                      o_send.at[k - 1, b], o_recv.at[k - 1, b], (dx, fz, t))

    def x_forward(lo, hi):
        def body(b):
            x_copy(0, b).wait_recv()
            x_copy(2, b).start()
        for_each(lo, hi, body)

    def norm(src, dst, row, lo, n):
        gains = jnp.concatenate([gbuf[j, row:row + 1, :] for j in range(NZ)], axis=-1).astype(jnp.float32)

        def body(i):
            h = src[at_rows(lo + i * BLK, BLK), :].astype(jnp.float32)
            inv = lax.rsqrt(jnp.mean(h * h, axis=-1, keepdims=True) + NORM_EPS)
            dst(i)[...] = (h * inv * gains).astype(jnp.bfloat16)

        for_each(0, n // BLK, body)

    def x_norm(part):
        if part == 0:
            for cp in g_copies():
                cp.wait_recv()
            g_own().wait()

        def body(b):
            x_copy(1, b).wait_recv()
            x_copy(2, b).wait_recv()
            x_copy(2, b).wait_send()
            x_own(b).wait()

        for_each(part * per, part * per + per, body)
        lo = part * per * SEQ
        norm(xa, lambda i: xa.at[at_rows(lo + i * BLK, BLK)], 0, lo, per * SEQ)

    def late_sends():
        def body(b):
            for k in range(2):
                x_copy(k, b).wait_send()
        for_each(0, ROWS, body)
        for cp in g_copies():
            cp.wait_send()
        res_load().wait()

    def piece(w, base, lo, width, slot, first, col):
        sh, g = shards[w], gathered[w]
        ks = sh.shape[0]
        cols = pl.ds(pl.multiple_of(lo, 128), width)
        out = []
        for j in range(NZ):
            src = sh.at[:, cols] if j == 0 else g.at[j, :, cols]
            at = pl.ds(pl.multiple_of(base + lax.rem(fz + j, NZ) * ks, 32), ks)
            out.append(pltpu.make_async_copy(src, wbuf.at[slot, at, col:col + width], wsem.at[slot, first + j]))
        return out

    def tiles(n, start, wait, compute):
        start(0, 0)

        def body(t):
            slot = lax.rem(t, 2)

            @pl.when(t + 1 < n)
            def _():
                start(t + 1, 1 - slot)

            wait(t, slot)
            compute(t, slot)

        for_each(0, n, body)

    def simple(n, load, compute):
        def start(t, slot):
            for cp in load(t, slot):
                cp.start()

        def wait(t, slot):
            for cp in load(t, slot):
                cp.wait()

        tiles(n, start, wait, compute)

    def by_rows(n, rows, body):
        for_each(0, n, lambda m: body(pl.ds(pl.multiple_of(m * rows, rows), rows)))

    m_rows = TOK // 2
    n_m = TOK // m_rows

    def qkv(part):
        rows = 2 * SEQ
        top = 3 * HEADS - 1

        def start(t, slot):
            for side in range(2):
                hh = jnp.minimum(2 * t + side, top)
                for j, w in enumerate((W_Q, W_K, W_V)):
                    @pl.when(lax.div(hh, HEADS) == j)
                    def _():
                        for cp in piece(w, 0, s * OWN + lax.rem(hh, HEADS) * 128, 128, slot, NZ * side, 128 * side):
                            cp.start()

        def wait(t, slot):
            for side in range(2):
                for cp in piece(W_Q, 0, s * OWN, 128, slot, NZ * side, 128 * side):
                    cp.wait()

        def compute(t, slot):
            def body(m):
                at = at_rows(part * per * SEQ + m * rows, rows)
                acc = jnp.dot(xa[at, :], wbuf[slot, 0:DIM, :], preferred_element_type=jnp.float32)
                cos, sin = cos_tab[...], sin_tab[...]
                for side in range(2):
                    p = acc[:, side * 128:(side + 1) * 128]
                    swapped = jnp.concatenate([p[:, 64:], p[:, :64]], axis=-1)
                    turned = 2 * t + side < 2 * HEADS
                    val = jnp.where(turned, p * cos + swapped * sin, p)
                    big[at, pl.ds(pl.multiple_of((2 * t + side) * 128, 128), 128)] = val.astype(jnp.bfloat16)

            for_each(0, per * SEQ // rows, body)

        tiles(8, start, wait, compute)

    def attention(part):
        def body(b):
            at = at_rows(b * SEQ, SEQ)
            for h in range(HEADS):
                q, k, v = (big[at, (j * HEADS + h) * 128:(j * HEADS + h + 1) * 128] for j in range(3))
                sc = lax.dot_general(q, k, (((1,), (1,)), ((), ())), preferred_element_type=jnp.float32)
                sc = jnp.where(keep[...] > 0, sc * HEAD_DIM ** -0.5, MASK_VALUE)
                e = jnp.exp(sc - jnp.max(sc, axis=-1, keepdims=True))
                tot = jnp.sum(e, axis=-1, keepdims=True)
                o = jnp.dot(e.astype(jnp.bfloat16), v, preferred_element_type=jnp.float32) / tot
                big[at, h * 128:(h + 1) * 128] = o.astype(jnp.bfloat16)

        for_each(part * per, part * per + per, body)

    def send_mix(part):
        def body(b):
            for k in range(1, SP):
                o_copy(k, b).start()
            mix[at_rows(b * BLK, BLK), pl.ds(pl.multiple_of(s * OWN, 128), OWN)] = big[at_rows(b * SEQ + s * BLK, BLK), 0:OWN]

        for_each(part * per, part * per + per, body)

    act_at = 3 * TOK

    def out_proj():
        def arrive(b):
            for k in range(1, SP):
                o_copy(k, b).wait_recv()
        for_each(0, ROWS, arrive)

        def load(t, slot):
            return piece(W_O, 0, t * TILE, TILE, slot, 0, 0)

        def compute(t, slot):
            cols = pl.ds(pl.multiple_of(t * TILE, 128), TILE)

            def body(at):
                acc = jnp.dot(mix[at, :], wbuf[slot, 0:DIM, :], preferred_element_type=jnp.float32)
                res[at, cols] = (res[at, cols].astype(jnp.float32) + acc).astype(jnp.bfloat16)

            by_rows(n_m, m_rows, body)

        simple(DIM // TILE, load, compute)
        norm(res, lambda i: xa.at[at_rows(act_at + i * BLK, BLK)], 1, 0, TOK)

        def gone(b):
            for k in range(1, SP):
                o_copy(k, b).wait_send()
        for_each(0, ROWS, gone)

    def gate_up(lo, width):
        def load(t, slot):
            return (piece(W_G, 0, lo + t * TILE, TILE, slot, 0, 0)
                    + piece(W_U, DIM, lo + t * TILE, TILE, slot, NZ, 0))

        def compute(t, slot):
            tile = lo // TILE + t
            blk = lax.div(tile, DIM // TILE)
            cols = pl.ds(pl.multiple_of(lax.rem(tile, DIM // TILE) * TILE, 128), TILE)

            def body(m):
                a = xa[pl.ds(pl.multiple_of(act_at + m * m_rows, m_rows), m_rows), :]
                g = jnp.dot(a, wbuf[slot, 0:DIM, :], preferred_element_type=jnp.float32)
                u = jnp.dot(a, wbuf[slot, DIM:2 * DIM, :], preferred_element_type=jnp.float32)
                at = pl.ds(pl.multiple_of(blk * TOK + m * m_rows, m_rows), m_rows)
                xa[at, cols] = (g / (1.0 + jnp.exp(-g)) * u).astype(jnp.bfloat16)

            for_each(0, n_m, body)

        simple(width // TILE, load, compute)

    def y_copy(t):
        cols = pl.ds(pl.multiple_of(t * TILE, 128), TILE)
        return pltpu.make_async_copy(mix.at[:, cols], y_out.at[:, cols], ysem.at[t])

    def down(lo, width):
        def load(t, slot):
            return piece(W_D, 0, lo + t * TILE, TILE, slot, 0, 0)

        def compute(t, slot):
            cols = pl.ds(pl.multiple_of(lo + t * TILE, 128), TILE)

            def body(m):
                acc = None
                for j in range(3):
                    n = min(DIM, FFN - j * DIM)
                    h = xa[pl.ds(pl.multiple_of(j * TOK + m * m_rows, m_rows), m_rows), 0:n]
                    d = jnp.dot(h, wbuf[slot, j * DIM:j * DIM + n, :], preferred_element_type=jnp.float32)
                    acc = d if acc is None else acc + d
                at = pl.ds(pl.multiple_of(m * m_rows, m_rows), m_rows)
                mix[at, cols] = (res[at, cols].astype(jnp.float32) + acc).astype(jnp.bfloat16)

            for_each(0, n_m, body)
            y_copy(lo // TILE + t).start()

        simple(width // TILE, load, compute)

    def begin(b):
        x_copy(0, b).start()
        x_copy(1, b).start()
        x_own(b).start()

    for cp in g_copies() + [g_own()]:
        cp.start()
    for_each(0, ROWS, begin)
    res_load().start()
    hooks = {}

    def hook(tick, fn, *args):
        hooks.setdefault(tick, []).append(functools.partial(fn, *args))

    last = {}
    for r, (w, lo, width) in enumerate(rounds):
        last[(w, lo)] = r + (2 if w <= W_V else LAG)
    for j, tick in enumerate(FORWARD_TICKS):
        hook(tick, x_forward, 3 * j, 3 * j + 3)
    tick = last[(W_V, 256)]
    for part in range(PARTS):
        hook(tick - 2 + part, x_norm, part)
    hook(tick, late_sends)
    for part in range(PARTS):
        hook(tick + part, qkv, part)
        hook(tick + part, attention, part)
        hook(tick + part, send_mix, part)
    tick = max(last[(W_O, HALF)], tick + PARTS + OUT_WAIT)
    hook(tick, out_proj)
    for w, lo, width in rounds:
        if w == W_U:
            tick = max(tick + 1, last[(w, lo)])
            hook(tick, gate_up, lo, width)
        if w == W_D:
            hook(last[(w, lo)], down, lo, width)
    for i in range(mv.ticks()):
        mv.step(i)
        for fn in hooks.get(i, ()):
            fn()
    for t in range(DIM // TILE):
        y_copy(t).wait()
    mv.finish()


def local_layer(x_loc, norm_attn, w_query, w_key, w_value, w_out, norm_mlp, w_gate, w_up, w_down):
    shards = (w_query, w_key, w_value, w_out, w_gate, w_up, w_down)
    gain = jnp.concatenate([norm_attn[None], norm_mlp[None], jnp.zeros((14, DIM // NZ), jnp.bfloat16)], axis=0)
    seq_idx = jnp.arange(SEQ, dtype=jnp.int32)
    pos = (seq_idx % BLK) * SP + seq_idx // BLK
    inv_freq = jnp.exp(jnp.arange(HEAD_DIM // 2, dtype=jnp.float32) * (-2.0 * math.log(ROPE_THETA) / HEAD_DIM))
    angles = pos.astype(jnp.float32)[:, None] * inv_freq[None, :]
    cos, sin = jnp.cos(angles), jnp.sin(angles)
    cos_tab = jnp.tile(jnp.concatenate([cos, cos], axis=-1), (2, 1))
    sin_tab = jnp.tile(jnp.concatenate([-sin, sin], axis=-1), (2, 1))
    keep = (pos[None, :] <= pos[:, None]).astype(jnp.float32)
    rounds, early = plan()
    any_spec = pl.BlockSpec(memory_space=pl.ANY)
    vmem_spec = pl.BlockSpec(memory_space=pltpu.VMEM)
    dma = pltpu.SemaphoreType.DMA
    bf16 = jnp.bfloat16
    outs = [jax.ShapeDtypeStruct((TOK, DIM), bf16)]
    outs += [jax.ShapeDtypeStruct((NZ,) + w.shape, bf16) for w in shards]
    res = pl.pallas_call(
        functools.partial(layer_kernel, rounds, early),
        out_shape=outs,
        in_specs=[any_spec, any_spec] + [vmem_spec] * 3 + [any_spec] * 7,
        out_specs=[any_spec] * 8,
        scratch_shapes=[
            pltpu.VMEM((ALL, DIM), bf16), pltpu.VMEM((ALL, 16 * 128), bf16), pltpu.VMEM((TOK, DIM), bf16),
            pltpu.VMEM((TOK, DIM), bf16), pltpu.VMEM((NZ, 16, DIM // NZ), bf16), pltpu.VMEM((2, FFN, TILE), bf16),
            dma((SLOTS, N_KINDS)), dma((SLOTS, N_KINDS)), dma((3, ROWS)), dma((3, ROWS)),
            dma((SP - 1, ROWS)), dma((SP - 1, ROWS)), dma((NZ - 1,)), dma((NZ - 1,)),
            dma((ROWS + 2,)), dma((2, 2 * NZ)), dma((DIM // TILE,))],
        compiler_params=pltpu.CompilerParams(has_side_effects=True, vmem_limit_bytes=60 * 1024 * 1024),
    )(x_loc.reshape(TOK, DIM), gain, cos_tab, sin_tab, keep, *shards)
    return res[0].reshape(x_loc.shape)


def solution(mesh):
    row_spec = P(('dp', 'fsdp'), 'sp', None)
    weight_spec = P('fsdp', None)
    gain_spec = P('fsdp')
    in_specs = (row_spec, gain_spec, weight_spec, weight_spec, weight_spec, weight_spec, gain_spec, weight_spec, weight_spec, weight_spec)
    return jax.shard_map(local_layer, mesh=mesh, in_specs=in_specs, out_specs=row_spec, check_vma=False)
```

time: 653 us -> 560 us (0.86)
  the two profiles are of different devices: /device:TPU:29 before, /device:TPU:0 now
where the time goes in v2:
time: 560 us
  Pallas kernels  551 us (98%)
  local copies, waits for them, and re-layouts  7.17 us (1%)
    pallas_call x1, Pallas kernels, local_layer(): pl.pallas_call(functools.partial(layer_kernel, rounds, early), out_shape=...  551 us

profile of v2, /device:TPU:0, one launch (start us, length us, event | category | flops | bytes accessed | tf_op | source)
XLA Modules:
  0.0 560.0 jit_solution(9842570767087308495)
XLA Ops:
  0.0 0.1 pad.6.clone
  0.1 0.7 broadcast_in_dim.6
  0.8 0.7 broadcast_in_dim.14
  1.5 0.7 maximum_maximum_fusion.gain
  2.2 0.8 compare_convert_fusion.keep
  3.0 0.5 fusion
  3.5 0.1 pad_maximum_fusion
  3.6 0.7 tile.8
  4.4 0.7 tile.20
  5.1 550.6 %shard_map.100 = (bf16[768,2560]{1,0:T(8,128)(2,1)}, bf16[4,640,2560]{2,1,0:T(8,128)(2,1)}, bf16[4,640,2560]{2,1,0:T(8,128)(2,1)}, bf16[4,640,2560]{2,1,0:T(8,12...) custom-call(bf16[768,2560]{1,0:T(8,128)(2,1)} %bitcast.5, ...), custom_call_target="tpu_custom_call" | custom-call | tf_op jit(solution)/shard_map/pallas_call | solution.py:542
  555.7 4.3 copy.12
  (4 shorter events, 0.0 us)

commit v3 on v2

--- a/solution.py
+++ b/solution.py
@@ -26,14 +26,14 @@
 HEADS = OWN // 128
 PARTS = 3
 OUT_WAIT = 1
-EARLY = 13
+EARLY = 11
 FORWARD_TICKS = (2, 4, 6, 7)
 GATE_WIDTHS = (1536, 1536, 1280, 1280, 768, 512)
-DOWN_WIDTHS = (768, 768, 512, 256, 256)
+DOWN_WIDTHS = (512, 512, 256, 256, 256, 256, 256, 256)
 TILE = 256
 N_KINDS = 16
 SLOTS = 12
-AHEAD = 3
+AHEAD = 2
 LAG = 5
 Z_STAGES = ('z1', 'z2', 'z3')
 W_Q, W_K, W_V, W_O, W_G, W_U, W_D = range(7)

time: 560 us -> 538 us (0.961)
  Pallas kernels: 551 us -> 528 us
    pallas_call x1, Pallas kernels: 551 us -> 528 us  [local_layer(): pl.pallas_call(functools.partial(layer_kernel, rounds, early), out_shape=...]
where the time goes in v3:
time: 538 us; the launch traced here: 537 us
  Pallas kernels  528 us (98%)
  local copies, waits for them, and re-layouts  7.17 us (1%)
    pallas_call x1, Pallas kernels, local_layer(): pl.pallas_call(functools.partial(layer_kernel, rounds, early), out_shape=...  528 us

profile of v3, /device:TPU:0, one launch (start us, length us, event | category | flops | bytes accessed | tf_op | source)
XLA Modules:
  0.0 537.5 jit_solution(6967225334189635087)
XLA Ops:
  0.0 0.1 pad.6.clone
  0.1 0.7 broadcast_in_dim.6
  0.8 0.7 broadcast_in_dim.14
  1.5 0.7 maximum_maximum_fusion.gain
  2.2 0.8 compare_convert_fusion.keep
  3.0 0.5 fusion
  3.5 0.1 pad_maximum_fusion
  3.6 0.7 tile.8
  4.4 0.7 tile.20
  5.1 528.1 %shard_map.100 = (bf16[768,2560]{1,0:T(8,128)(2,1)}, bf16[4,640,2560]{2,1,0:T(8,128)(2,1)}, bf16[4,640,2560]{2,1,0:T(8,128)(2,1)}, bf16[4,640,2560]{2,1,0:T(8,12...) custom-call(bf16[768,2560]{1,0:T(8,128)(2,1)} %bitcast.5, ...), custom_call_target="tpu_custom_call" | custom-call | tf_op jit(solution)/shard_map/pallas_call | solution.py:542
  533.2 4.3 copy.12
  (4 shorter events, 0.0 us)
